TPU v7x, 128 devices: a whole 4x4x4 slice. The times are simulated.
128 devices in a mesh: path: 32 (over z_hi, y, x), tm: 4 (over z_lo, core).
Axes of the slice: x: 4, y: 4, z: 4 (z_hi: 2, z_lo: 2; z = z_hi * 2 + z_lo), core: 2. Of those that a mesh axis runs over, the one named last changes fastest.
Arguments:
- increments: bfloat16 [32768, 32, 1000], P(('path', 'tm')), may hold values from -6 to 6
- level_table: int32 [16384], replicated, may hold values from 0 to 4, as said below
- time_table: int32 [16384], replicated, may hold values from 0 to 31, as said below
Outputs:
- value_est: float32 [32], P('tm')
- grad_est: float32 [32, 1000], P('tm')
Inputs may be any that keep to these rules, and one draw needn't show every extreme that they name: `level_table`: never falls from one block to the next. `time_table`: split the 32 time points into as many runs of consecutive points as the tm axis has devices; the 128 consecutive entries of each device fall equally into every run.
All inputs are finite; a program needn't handle non-finite values.
Results may differ from a plain program's by a relative error of at most 0.0003.
The roundings to bfloat16 on the way count: a program that leaves them out, or rounds other values in their place, can miss the bound.
Values may be sent and summed in bfloat16 or wider, within the bound.
A program may use at most 128 MiB of HBM per device.

v0:
```python
import jax
import jax.numpy as jnp
from jax import lax
from jax.sharding import PartitionSpec as P

LEVELS = 5
BLOCK = 2


horizon = 0.3


def in_blocks(array, dim, peers):
    shape = array.shape
    blocks = array.reshape(*shape[:dim], peers, shape[dim] // peers, *shape[dim + 1 :])
    return jnp.moveaxis(blocks, dim, 0)


def sent_and_summed(array, axis, dim):
    blocks = in_blocks(array, dim, lax.axis_size(axis))
    arrived = lax.all_to_all(blocks, axis, split_axis=0, concat_axis=0, tiled=True)
    return arrived.sum(axis=0)


def copy_for_each(array, axis):
    peers = lax.axis_size(axis)
    return lax.all_to_all(
        jnp.broadcast_to(array[None], (peers, *array.shape)), axis, 0, 0, tiled=True
    )


def of_everyone(array, axis):
    return copy_for_each(array, axis).sum(axis=0)


def together(arrays, axis):
    vector, at, done = (jnp.concatenate([a.reshape(-1) for a in arrays]), 0, [])
    subtotal = of_everyone(vector, axis)
    for a in arrays:
        done.append(subtotal[at : at + a.size].reshape(a.shape))
        at += a.size
    return tuple(done)


def stride_weights(levels, starts, steps_k, step_len):
    steps = jnp.arange(steps_k)
    fine_stride = jnp.power(2, LEVELS - 1 - levels).astype(jnp.int32)
    coarse = fine_stride * 2
    live_steps = steps[None, :] >= starts[:, None]
    on_fine = steps[None, :] % fine_stride[:, None] == 0
    on_coarse = (steps[None, :] % coarse[:, None] == 0) & (levels[:, None] > 0)
    term = fine_stride[:, None] * on_fine.astype(jnp.int32) - coarse[:, None] * on_coarse.astype(
        jnp.int32
    )
    return step_len * (live_steps.astype(jnp.float32) * term.astype(jnp.float32))


def terminal(incr, starts):
    steps_k = incr.shape[1]
    width = incr.shape[2]
    step_len = horizon / steps_k
    steps = jnp.arange(steps_k)
    live_steps = (steps[None, :] >= starts[:, None]).astype(jnp.bfloat16)
    end_point = jnp.sqrt(step_len) * jnp.einsum(
        "pi,pid->pd", live_steps, incr, preferred_element_type=jnp.float32
    )
    remaining = horizon - starts.astype(jnp.float32) * step_len
    scaled = end_point / remaining[:, None]
    end_value = 1.0 / (2.0 + 0.4 * jnp.sum(end_point * end_point, axis=1) / width)
    return (scaled, end_value)


def partial_sums(path_total, scaled, row_index, path_share, row_count):
    select = (row_index[:, None] == jnp.arange(row_count)[None, :]).astype(jnp.float32)
    select = select * (path_share * path_total)[:, None]
    return (jnp.sum(select, axis=0), jnp.dot(select.T, scaled, precision=lax.Precision.HIGHEST))


def first_terms(incr, levels, starts, path_share, row_count, offset):
    scaled, end_value = terminal(incr, starts)
    path_total = end_value * (levels == 0).astype(jnp.float32)
    return partial_sums(path_total, scaled, starts - offset, path_share, row_count)


def second_terms(incr, levels, starts, path_share, value_one, grad_low, row_count, offset):
    paths, steps_k, width = incr.shape
    step_len = horizon / steps_k
    scaled, end_value = terminal(incr, starts)
    inner_dots = jnp.dot(
        incr.reshape(paths * steps_k, width), grad_low.T, preferred_element_type=jnp.float32
    ).reshape(paths, steps_k, steps_k)
    steps = jnp.arange(steps_k)
    window = (steps[None, :, None] >= starts[:, None, None]) & (
        steps[None, :, None] < steps[None, None, :]
    )
    estimate = value_one[None, :] + jnp.sqrt(step_len) * jnp.sum(
        inner_dots * window.astype(jnp.float32), axis=1
    )
    drift_term = estimate - estimate * estimate * estimate
    weights = stride_weights(levels, starts, steps_k, step_len)
    path_total = end_value * (levels == 0).astype(jnp.float32) + jnp.sum(
        weights * drift_term, axis=1
    )
    return partial_sums(path_total, scaled, starts - offset, path_share, row_count)


def shards(increments, level_table, time_table):
    groups = lax.axis_size("tm")
    devices = lax.axis_size("path") * groups
    my_index = lax.axis_index("path") * groups + lax.axis_index("tm")
    blk_dev = level_table.shape[0] // devices
    steps_k = increments.shape[1]
    lvl_hot = (level_table[:, None] == jnp.arange(LEVELS)[None, :]).astype(jnp.float32)
    time_hot = (time_table[:, None] == jnp.arange(steps_k)[None, :]).astype(jnp.float32)
    counts = jnp.dot(lvl_hot.T, time_hot, precision=lax.Precision.HIGHEST)
    own_levels = lax.dynamic_slice_in_dim(level_table, my_index * blk_dev, blk_dev)
    own_times = lax.dynamic_slice_in_dim(time_table, my_index * blk_dev, blk_dev)
    lvl_path = jnp.repeat(own_levels, BLOCK)
    time_path = jnp.repeat(own_times, BLOCK)
    path_share = 1.0 / (BLOCK * counts[lvl_path, time_path])
    value_one, grad_one = lax.psum(
        first_terms(increments, lvl_path, time_path, path_share, steps_k, 0), ("path", "tm")
    )
    grad_low = grad_one.astype(jnp.bfloat16)
    value_part, grad_part = jax.tree.map(
        lambda part: sent_and_summed(part, "tm", 0),
        second_terms(increments, lvl_path, time_path, path_share, value_one, grad_low, steps_k, 0),
    )
    value_est, grad_est = together((value_part, grad_part), "path")
    return (value_est, grad_est)


def solution(mesh):
    placed = (P(("path", "tm"), None, None), P(), P())
    return jax.shard_map(
        shards, mesh=mesh, in_specs=placed, out_specs=(P("tm"), P("tm", None)), check_vma=False
    )
```

profile of v0, /device:TPU:1, one launch (start us, length us, event | category | flops | bytes accessed | tf_op | source)
XLA Modules:
  0.0 165.2 jit_solution(9377580538771082591)
XLA Ops:
  0.6 0.8 broadcast_compare_fusion
  1.4 0.8 dynamic_slice.6
  2.2 1.4 fusion
  3.6 0.2 reshape.302
  4.0 0.1 reshape.301
  4.3 23.5 %copy.17 = bf16[256,32,1000]{2,1,0:T(8,128)(2,1)} copy(bf16[256,32,1000]{0,2,1:T(8,128)(2,1)} %param.5) | data formatting | bytes 32768000 | tf_op args[0]
  27.7 7.1 %multiply_reduce_fusion = f32[256,1000]{0,1:T(8,128)S(1)} fusion(bf16[256,32,1000]{0,2,1:T(8,128)(2,1)} %param.5, f32[256,32]{0,1:T(8,128)S(1)} %get-tuple-element.16), kind=kLoop, calls=%fused_computation.1 | loop fusion | flops 24320000 | bytes 17440768 | tf_op jit(solution)/shard_map/pi,pid->pd/dot_general | solution.py:64
  34.8 0.2 multiply_reduce_fusion.1
  35.1 0.1 eq.85
  35.2 1.4 gather_fusion
  36.8 1.0 fusion.2
  37.7 69.6 %all-reduce = (bf16[32,1000]{1,0:T(8,128)(2,1)S(1)}, f32[32]{0:T(128)S(1)}) all-reduce(f32[32,1000]{1,0:T(8,128)S(1)} %fusion.2, f32[32]{0:T(128)S(1)} %select_reduce_fusion.2), channel_id=1, replica_groups=mesh['path'=32,'tm'=4] {'path','tm'}, use_global_device_ids=true, to_apply=%region_3.5 | all-reduce | flops 32032 | bytes 192256 | tf_op jit(solution)/shard_map/psum | solution.py:121
  107.3 10.7 %convolution_bitcast_fusion = f32[8192,32]{0,1:T(8,128)S(1)} fusion(bf16[8192,1000]{1,0:T(8,128)(2,1)} %bitcast.13, bf16[32,1000]{1,0:T(8,128)(2,1)S(1)} %get-tuple-element.3), kind=kOutput, calls=%fused_computation.2 | convolution fusion | flops 524288000 | bytes 17496576 | tf_op jit(solution)/shard_map/dot_general | solution.py:89
  118.0 2.7 %reshape.304 = f32[256,32,32]{1,0,2:T(8,128)} reshape(f32[8192,32]{0,1:T(8,128)S(1)} %convolution_bitcast_fusion) | data formatting | bytes 2097152 | tf_op jit(solution)/shard_map/reshape | solution.py:91
  121.0 0.1 reshape.323
  121.2 0.1 reshape.325
  121.4 0.1 ne.146
  121.7 0.1 reshape.313
  122.1 0.2 select_n.157
  122.5 3.3 %select_reduce_fusion = f32[256,32]{0,1:T(8,128)S(1)} fusion(f32[256,32,32]{1,0,2:T(8,128)} %reshape.304, pred[32,32]{0,1:T(8,128)(4,1)S(1)} %iota_compare_fusion.8, pred[256,32]{1,0:T(8,128)(4,1)S(1)} %copy.16), kind=kLoop, calls=%fused_computation.3 | loop fusion | flops 778240 | bytes 1090560 | tf_op jit(solution)/shard_map/reduce_sum | solution.py:96
  125.9 0.7 fusion.8
  126.7 0.7 all_to_all.13
  127.4 4.1 %all-to-all-start = ((f32[4,1,8]{2,1,0:T(1,128)}), f32[4,1,8]{2,1,0:T(1,128)S(1)}, u32[]{:S(2)}, u32[]{:S(2)}) async-start(f32[4,1,8]{2,1,0:T(1,128)} %bitcast.5), calls=%async_computation | async-start | bytes 4096 | tf_op jit(solution)/shard_map/all_to_all | solution.py:21
  131.5 1.6 convolution_bitcast_fusion.1
  133.1 1.4 all-to-all-done
  134.5 4.0 %all-to-all-start.1 = ((f32[4,8,1000]{2,1,0:T(8,128)}), f32[4,8,1000]{2,1,0:T(8,128)S(1)}, u32[]{:S(2)}, u32[]{:S(2)}) async-start(f32[4,8,1000]{2,1,0:T(8,128)} %convolution_bitcast_fusion.1), calls=%async_computation.1 | async-start | bytes 262144 | tf_op jit(solution)/shard_map/all_to_all | solution.py:21
  138.5 3.5 %all-to-all-done.1 = f32[4,8,1000]{2,1,0:T(8,128)S(1)} async-done(((f32[4,8,1000]{2,1,0:T(8,128)}), f32[4,8,1000]{2,1,0:T(8,128)S(1)}, u32[]{:S(2)}, u32[]{:S(2)}) %all-to-all-start.1) | async-done | bytes 128032 | tf_op jit(solution)/shard_map/all_to_all | solution.py:21
  142.2 0.5 broadcast_in_dim.33
  142.8 20.5 %all_to_all.20 = f32[32,1,8008]{2,1,0:T(1,128)S(1)} all-to-all(f32[32,1,8008]{2,1,0:T(1,128)S(1)} %broadcast_in_dim.33), channel_id=1, replica_groups=mesh['path'=32,'tm'=4] {'path'}, dimensions={0} | all-to-all | bytes 2050048 | tf_op jit(solution)/shard_map/all_to_all | solution.py:27
  163.3 0.6 reduce_sum.83
  164.0 0.5 slice.10
  164.5 0.7 reshape.307
  (33 shorter events, 2.0 us)
Async XLA Ops:
  127.4 7.1 %all-to-all-start = ((f32[4,1,8]{2,1,0:T(1,128)}), f32[4,1,8]{2,1,0:T(1,128)S(1)}, u32[]{:S(2)}, u32[]{:S(2)}) async-start(f32[4,1,8]{2,1,0:T(1,128)} %bitcast.5), calls=%async_computation | async-start | bytes 4096 | tf_op jit(solution)/shard_map/all_to_all | solution.py:21
  134.5 7.6 %all-to-all-start.1 = ((f32[4,8,1000]{2,1,0:T(8,128)}), f32[4,8,1000]{2,1,0:T(8,128)S(1)}, u32[]{:S(2)}, u32[]{:S(2)}) async-start(f32[4,8,1000]{2,1,0:T(8,128)} %convolution_bitcast_fusion.1), calls=%async_computation.1 | async-start | bytes 262144 | tf_op jit(solution)/shard_map/all_to_all | solution.py:21
where the time goes:
time: 167 us; the launch traced here: 165 us
  blocking collectives  90.1 us (54%)
  local copies, waits for them, and re-layouts  33.5 us (20%)
  matrix products  14.6 us (9%)
  other arithmetic  13.1 us (8%)
  starting transfers between devices  8.04 us (5%)
  waiting for transfers between devices  4.94 us (3%)
    psum x1, blocking collectives, shards(): lax.psum(first_terms(increments, lvl_path, time_path, path_share, steps_k...  69.6 us
    unnamed x1, local copies, waits for them, and re-layouts  23.5 us
    all_to_all x1, blocking collectives, copy_for_each(): lax.all_to_all(jnp.broadcast_to(array[None], (peers, *array.shape)), axis...  20.5 us
    dot_general x1, matrix products, second_terms(): jnp.dot(incr.reshape(paths * steps_k, width), grad_low.T, preferred_eleme...  10.7 us
    all_to_all x2, starting transfers between devices, sent_and_summed(): lax.all_to_all(blocks, axis, split_axis=0, concat_axis=0, tiled=True)  8.04 us
    dot_general x1, other arithmetic, terminal(): jnp.einsum('pi,pid->pd', live_steps, incr, preferred_element_type=jnp.flo...  7.07 us
    all_to_all x2, waiting for transfers between devices, sent_and_summed(): lax.all_to_all(blocks, axis, split_axis=0, concat_axis=0, tiled=True)  4.94 us
    reduce_sum x1, other arithmetic, second_terms(): jnp.sum(inner_dots * window.astype(jnp.float32), axis=1)  3.35 us
  transfers between devices with their start and end apart: 2, of which 2 were waited for; matrix products, arithmetic and copies ran while one was open for 1% of the time, Pallas kernels for 0%

commit v1 on v0

v1 whole, which is shorter than its diff:
```python
import functools
import itertools

import jax
import jax.numpy as jnp
from jax import lax
from jax.experimental import pallas as pl
from jax.experimental.pallas import tpu as pltpu
from jax.sharding import PartitionSpec as P

LEVELS = 5
HORIZON = 0.3
MESH = pl.DeviceIdType.MESH
HIGHEST = lax.Precision.HIGHEST
SIDE = 4
GROUPS = (8, 8, 8, 4, 2, 2)


def reach(offset):
    return sum(min(d, SIDE - d) for d in offset)


def opposite(offset):
    return tuple((d + 2) % SIDE for d in offset)


def near(offset):
    other = opposite(offset)
    return (reach(offset), offset) < (reach(other), other)


OFFSETS = sorted(itertools.product(range(SIDE), repeat=3), key=lambda o: -reach(o))
NEAR = [o for o in OFFSETS if near(o)]
NEAR_PATH = [o for o in NEAR if o[0] % 2 == 0]


class Place:
    def __init__(self):
        self.path, self.tm = lax.axis_index("path"), lax.axis_index("tm")
        self.me = self.path * 4 + self.tm
        z_hi, y, x = self.path // 16, lax.rem(self.path // 4, 4), lax.rem(self.path, 4)
        z, core = z_hi * 2 + self.tm // 2, lax.rem(self.tm, 2)
        zs = [lax.rem(z + d, SIDE) for d in range(SIDE)]
        ys = [lax.rem(y + d, SIDE) for d in range(SIDE)]
        xs = [lax.rem(x + d, SIDE) for d in range(SIDE)]
        self.high = [q // 2 for q in zs]
        self.low = [lax.rem(q, 2) * 2 for q in zs]
        self.ys, self.xs = ys, xs
        self.cores = [core, 1 - core]
        turned_y = [lax.rem(q + 2, SIDE) for q in ys]
        turned_x = [lax.rem(q + 2, SIDE) for q in xs]
        self.turned_y, self.turned_x = turned_y, turned_x

    def peer(self, offset, core):
        dz, dy, dx = offset
        return (self.high[dz] * 16 + self.ys[dy] * 4 + self.xs[dx], self.low[dz] + self.cores[core])

    def piece(self, offset):
        dz, dy, dx = offset
        high = self.high[dz]
        at_y = self.ys[dy] + high * (self.turned_y[dy] - self.ys[dy])
        at_x = self.xs[dx] + high * (self.turned_x[dx] - self.xs[dx])
        return at_y * 4 + at_x

    def peers(self, offsets, cores=(0, 1)):
        for offset in offsets:
            for core in cores:
                if offset != (0, 0, 0) or core:
                    yield offset, self.peer(offset, core)


def wait_all(count, ref, sem, place, sent):
    window = ref.at[pl.ds(0, count)]
    copy = pltpu.make_async_remote_copy(
        src_ref=window, dst_ref=window, send_sem=sem, recv_sem=sem,
        device_id=(place.path, place.tm), device_id_type=MESH,
    )
    if sent:
        copy.wait_send()
    else:
        copy.wait_recv()


def kernel(
    inc_hbm, lvl_ref, time_ref, value_ref, grad_ref,
    inc, end, mask, whole, mine, scattered, arrived, total, gathered,
    load_sem, scatter_send, scatter_recv, gather_send, gather_recv,
):
    steps_k, width, paths = inc.shape
    step_len = HORIZON / steps_k
    root = jnp.sqrt(jnp.float32(step_len))
    place = Place()
    devices = 128

    loads = [pltpu.make_async_copy(inc_hbm.at[i], inc.at[i], load_sem.at[i]) for i in range(steps_k)]
    for load in loads:
        load.start()
    barrier = pltpu.get_barrier_semaphore()
    for _, peer in place.peers(OFFSETS):
        pl.semaphore_signal(barrier, inc=1, device_id=peer, device_id_type=MESH)

    row_of = lax.broadcasted_iota(jnp.int32, (8, 128), 0)
    own_lvl = lvl_ref[pl.ds(place.me, 1), :].astype(jnp.float32)
    own_time = time_ref[pl.ds(place.me, 1), :].astype(jnp.float32)
    both = jnp.where(row_of == 0, own_lvl, own_time).astype(jnp.bfloat16)
    spread = (
        lax.broadcasted_iota(jnp.int32, (128, paths), 1) // 2
        == lax.broadcasted_iota(jnp.int32, (128, paths), 0)
    ).astype(jnp.float32).astype(jnp.bfloat16)
    per_path = jnp.dot(both, spread, preferred_element_type=jnp.float32)
    lvl, start = per_path[0:1], per_path[1:2]
    start_16 = jnp.broadcast_to(start, (16, paths))
    for i in range(steps_k):
        mask[i] = jnp.where(start_16 <= i, 1.0, 0.0).astype(jnp.bfloat16)

    step_row = lax.broadcasted_iota(jnp.int32, (steps_k, 128), 0)
    counts = [jnp.zeros((steps_k, 128), jnp.int32) for _ in range(LEVELS)]
    for part in range(4):
        packed = jnp.zeros((steps_k, 128), jnp.int32)
        for r in range(part * 32, part * 32 + 32):
            unit = jnp.left_shift(jnp.int32(1), 6 * lvl_ref[pl.ds(r, 1), :])
            packed = packed + jnp.where(time_ref[pl.ds(r, 1), :] == step_row, unit, 0)
        counts = [c + (jnp.right_shift(packed, 6 * n) & 63) for n, c in enumerate(counts)]
    shares = [
        1.0 / (2.0 * jnp.sum(c.astype(jnp.float32), axis=1, keepdims=True)) for c in counts
    ]
    step_at = lax.broadcasted_iota(jnp.int32, (steps_k, paths), 0)
    step_f = step_at.astype(jnp.float32)
    share = jnp.broadcast_to(shares[-1], (steps_k, paths))
    for n in range(LEVELS - 1):
        share = jnp.where(lvl == n, shares[n], share)
    share = jnp.where(start == step_f, share, 0.0)
    scale = root / (HORIZON - step_f[:, 0:1] * step_len)

    first_slab = 0
    for size in GROUPS:
        slabs = range(first_slab, first_slab + size)
        for i in slabs:
            loads[i].wait()
        masks = [mask[i] for i in slabs]

        def add(at, rows, slabs=slabs, masks=masks):
            terms = [
                (inc[i, pl.ds(at, rows), :] * jnp.concatenate([m] * (rows // 16), axis=0) if rows >= 16
                 else inc[i, pl.ds(at, rows), :] * m[0:rows]).astype(jnp.float32)
                for i, m in zip(slabs, masks)
            ]
            while len(terms) > 1:
                terms = [a + b for a, b in zip(terms[::2], terms[1::2])]
            if slabs[0]:
                end[pl.ds(at, rows), :] += terms[0]
            else:
                end[pl.ds(at, rows), :] = terms[0]

        @pl.loop(0, width // 32)
        def _(n):
            add(pl.multiple_of(n * 32, 32), 32)

        add(width // 32 * 32, width % 32)
        first_slab += size
    end[pl.ds(width, end.shape[0] - width), :] = jnp.zeros((end.shape[0] - width, paths), jnp.float32)

    ends = end[...]
    scaled = root * ends
    norm = jnp.sum(scaled * scaled, axis=0, keepdims=True)
    end_value = 1.0 / (2.0 + 0.4 * norm / width)
    first = jnp.where(lvl == 0.0, end_value, 0.0)

    def partial_sums(path_total, at):
        select = share * path_total
        grads = lax.dot_general(
            select * scale, end[...], (((1,), (1,)), ((), ())),
            precision=HIGHEST, preferred_element_type=jnp.float32,
        )
        values = jnp.sum(select, axis=1, keepdims=True)
        column = lax.broadcasted_iota(jnp.int32, grads.shape, 1)
        grads = jnp.where(column == width, values, grads)
        for t, c, r in itertools.product(range(4), range(8), range(2)):
            mine[at, t * 16 + c * 2 + r] = grads[8 * t + 4 * r : 8 * t + 4 * r + 4, 128 * c : 128 * c + 128]

    def scatter(at):
        for offset, (path, tm) in place.peers(OFFSETS):
            pltpu.make_async_remote_copy(
                src_ref=mine.at[at, tm * 16 + place.piece(offset)], dst_ref=scattered.at[at, place.me],
                send_sem=scatter_send.at[at], recv_sem=scatter_recv.at[at],
                device_id=(path, tm), device_id_type=MESH,
            ).start()
        scattered[at, place.me] = mine[at, place.tm * 16 + place.piece((0, 0, 0))]

    def added(at):
        wait_all(devices - 1, scattered.at[at], scatter_recv.at[at], place, False)
        return jnp.sum(scattered[at], axis=0)

    def gather(at, subtotal, offsets, cores, slot, home):
        total[at] = subtotal
        peers = list(place.peers(offsets, cores))
        for _, peer in peers:
            pltpu.make_async_remote_copy(
                src_ref=total.at[at], dst_ref=home.at[slot],
                send_sem=gather_send.at[at], recv_sem=gather_recv.at[at],
                device_id=peer, device_id_type=MESH,
            ).start()
        home[slot] = subtotal
        wait_all(len(peers), home, gather_recv.at[at], place, False)
        return len(peers)

    partial_sums(first, 0)
    pl.semaphore_wait(barrier, devices - 1)
    scatter(0)

    fine = jnp.where(lvl == 0.0, 16, jnp.where(lvl == 1.0, 8, jnp.where(lvl == 2.0, 4, jnp.where(lvl == 3.0, 2, 1))))
    on_fine = (step_at & (fine - 1)) == 0
    on_coarse = ((step_at & (2 * fine - 1)) == 0) & (lvl > 0.0)
    fine_f = fine.astype(jnp.float32)
    weight = step_len * (jnp.where(on_fine, fine_f, 0.0) - jnp.where(on_coarse, 2.0 * fine_f, 0.0))
    weight = jnp.where(step_f >= start, weight, 0.0)

    own = place.piece((0, 0, 0))
    sent = gather(0, added(0), NEAR, (0, 1), place.tm * 16 + own, arrived)
    for t, c, r in itertools.product(range(4), range(8), range(2)):
        whole[8 * t + 4 * r : 8 * t + 4 * r + 4, 128 * c : 128 * c + 128] = arrived[t * 16 + c * 2 + r]
    value_one = whole[:, width : width + 1]
    grad_low = whole[:, 0:width].astype(jnp.bfloat16)

    inner = jnp.zeros((steps_k, paths), jnp.float32)
    for i in range(steps_k - 1):
        dots = jnp.dot(grad_low, inc[i], preferred_element_type=jnp.float32)
        inner = inner + jnp.where((start <= i) & (step_at > i), dots, 0.0)
    estimate = value_one + root * inner
    drift = estimate - estimate * estimate * estimate
    second = first + jnp.sum(weight * drift, axis=0, keepdims=True)
    partial_sums(second, 1)
    scatter(1)
    gather_one = sent
    sent = gather(1, added(1), NEAR_PATH, (0,), own, gathered)
    for c, r in itertools.product(range(8), range(2)):
        whole[4 * r : 4 * r + 4, 128 * c : 128 * c + 128] = gathered[c * 2 + r]
    out = whole[0:8, :]
    grad_ref[...] = out[:, 0:width]
    eye = lax.broadcasted_iota(jnp.int32, (8, 8), 0) == lax.broadcasted_iota(jnp.int32, (8, 8), 1)
    value_ref[...] = jnp.sum(jnp.where(eye, out[:, width : width + 1], 0.0), axis=0, keepdims=True)

    for at in range(2):
        wait_all(devices - 1, scattered.at[at], scatter_send.at[at], place, True)
    wait_all(gather_one, arrived, gather_send.at[0], place, True)
    wait_all(sent, gathered, gather_send.at[1], place, True)


def shards(increments, level_table, time_table):
    paths, steps_k, width = increments.shape
    slabs = jnp.transpose(increments, (1, 2, 0))
    value, grad = pl.pallas_call(
        kernel,
        out_shape=(
            jax.ShapeDtypeStruct((1, 8), jnp.float32),
            jax.ShapeDtypeStruct((8, width), jnp.float32),
        ),
        in_specs=[
            pl.BlockSpec(memory_space=pl.ANY),
            pl.BlockSpec(memory_space=pltpu.VMEM),
            pl.BlockSpec(memory_space=pltpu.VMEM),
        ],
        out_specs=(pl.BlockSpec(memory_space=pltpu.VMEM), pl.BlockSpec(memory_space=pltpu.VMEM)),
        scratch_shapes=[
            pltpu.VMEM((steps_k, width, paths), jnp.bfloat16),
            pltpu.VMEM((1024, paths), jnp.float32),
            pltpu.VMEM((steps_k, 16, paths), jnp.bfloat16),
            pltpu.VMEM((steps_k, 1024), jnp.float32),
            pltpu.VMEM((2, 64, 4, 128), jnp.float32),
            pltpu.VMEM((2, 128, 4, 128), jnp.float32),
            pltpu.VMEM((64, 4, 128), jnp.float32),
            pltpu.VMEM((2, 4, 128), jnp.float32),
            pltpu.VMEM((16, 4, 128), jnp.float32),
            pltpu.SemaphoreType.DMA((steps_k,)),
            pltpu.SemaphoreType.DMA((2,)),
            pltpu.SemaphoreType.DMA((2,)),
            pltpu.SemaphoreType.DMA((2,)),
            pltpu.SemaphoreType.DMA((2,)),
        ],
        compiler_params=pltpu.CompilerParams(
            collective_id=0, has_side_effects=True, vmem_limit_bytes=48 * 1024 * 1024
        ),
    )(slabs, level_table.reshape(128, 128), time_table.reshape(128, 128))
    return (value.reshape(8), grad)


def solution(mesh):
    placed = (P(("path", "tm"), None, None), P(), P())
    return jax.shard_map(
        shards, mesh=mesh, in_specs=placed, out_specs=(P("tm"), P("tm", None)), check_vma=False
    )
```

time: 167 us -> 43.3 us (0.26)
  blocking collectives: 90.1 us -> 0 us
  Pallas kernels: 0 us -> 39.6 us
  local copies, waits for them, and re-layouts: 33.5 us -> 2.8 us
  matrix products: 14.6 us -> 0 us
  other arithmetic: 13.1 us -> 0 us
  starting transfers between devices: 8.04 us -> 0 us
  waiting for transfers between devices: 4.94 us -> 0 us
    psum x1 -> x0, blocking collectives: 69.6 us -> none  [shards(): lax.psum(first_terms(increments, lvl_path, time_path, path_share, steps_k...]
    pallas_call x0 -> x1, Pallas kernels: none -> 39.6 us  [shards(): pl.pallas_call(kernel, out_shape=(jax.ShapeDtypeStruct((1, 8), jnp.float3...]
    unnamed x1 -> x6, local copies, waits for them, and re-layouts: 23.5 us -> 2.8 us
    all_to_all x1 -> x0, blocking collectives: 20.5 us -> none  [copy_for_each(): lax.all_to_all(jnp.broadcast_to(array[None], (peers, *array.shape)), axis...]
    dot_general x4 -> x0, matrix products: 14.6 us -> none  [the longest x1 10.7 us: second_terms(): jnp.dot(incr.reshape(paths * steps_k, width), grad_low.T, preferred_eleme...]
    all_to_all x2 -> x0, starting transfers between devices: 8.04 us -> none  [sent_and_summed(): lax.all_to_all(blocks, axis, split_axis=0, concat_axis=0, tiled=True)]
    dot_general x1 -> x0, other arithmetic: 7.07 us -> none  [terminal(): jnp.einsum('pi,pid->pd', live_steps, incr, preferred_element_type=jnp.flo...]
    reduce_sum x8 -> x0, other arithmetic: 5.07 us -> none  [the longest x1 3.35 us: second_terms(): jnp.sum(inner_dots * window.astype(jnp.float32), axis=1)]
  transfers between devices with their start and end apart: 2 -> 0, of which waited for: 2 -> 0; matrix products, arithmetic and copies ran while one was open for 1% -> 0% of each run, Pallas kernels for 0% -> 0%
where the time goes in v1:
time: 43.3 us; the launch traced here: 43.1 us
  Pallas kernels  39.6 us (91%)
  local copies, waits for them, and re-layouts  2.8 us (6%)
  between operations  0.65 us (2%)
    pallas_call x1, Pallas kernels, shards(): pl.pallas_call(kernel, out_shape=(jax.ShapeDtypeStruct((1, 8), jnp.float3...  39.6 us
    unnamed x6, local copies, waits for them, and re-layouts  2.8 us

profile of v1, /device:TPU:1, one launch (start us, length us, event | category | flops | bytes accessed | tf_op | source)
XLA Modules:
  0.0 43.1 jit_solution(12355896266148404829)
XLA Ops:
  0.6 0.0 copy-start
  0.6 0.8 %copy-done = s32[16384]{0:T(1024)S(1)} copy-done((s32[16384]{0:T(1024)S(1)}, s32[16384]{0:T(1024)}, u32[]{:S(2)}) %copy-start) | copy-done | bytes 65560
  1.5 0.0 copy-start.1
  1.5 0.8 %copy-done.1 = s32[16384]{0:T(1024)S(1)} copy-done((s32[16384]{0:T(1024)S(1)}, s32[16384]{0:T(1024)}, u32[]{:S(2)}) %copy-start.1) | copy-done | bytes 65560
  2.3 39.6 %shard_map.50 = (f32[1,8]{1,0:T(1,128)S(1)}, f32[8,1000]{1,0:T(8,128)S(1)}) custom-call(bf16[32,1000,256]{2,1,0:T(8,128)(2,1)} %bitcast.7, s32[128,128]{1,0:T(8,128)S(1)} %bitcast.4, s32[128,128]{1,0:T(8,128)S(1)} %bitcast.5), custom_call_target="tpu_custom_call" | custom-call | tf_op jit(solution)/shard_map/pallas_call | solution.py:252
  41.9 0.5 %copy.7 = f32[8]{0:T(128)} copy(f32[8]{0:T(128)S(1)} %bitcast.6) | data formatting | bytes 64
  42.5 0.6 %copy.8 = f32[8,1000]{1,0:T(8,128)} copy(f32[8,1000]{1,0:T(8,128)S(1)} %get-tuple-element.9) | data formatting | bytes 64000
Async XLA Ops:
  0.6 0.8 %copy-start = (s32[16384]{0:T(1024)S(1)}, s32[16384]{0:T(1024)}, u32[]{:S(2)}) copy-start(s32[16384]{0:T(1024)} %param.4) | copy-start | bytes 196612
  1.5 0.8 %copy-start.1 = (s32[16384]{0:T(1024)S(1)}, s32[16384]{0:T(1024)}, u32[]{:S(2)}) copy-start(s32[16384]{0:T(1024)} %param.5) | copy-start | bytes 196612

commit v2 on v1

v2 whole, which is shorter than its diff:
```python
import functools
import itertools

import jax
import jax.numpy as jnp
from jax import lax
from jax.experimental import pallas as pl
from jax.experimental.pallas import tpu as pltpu
from jax.sharding import PartitionSpec as P

LEVELS = 5
HORIZON = 0.3
MESH = pl.DeviceIdType.MESH
HIGHEST = lax.Precision.HIGHEST
SIDE = 4
GROUPS = (8, 8, 8, 4, 3, 1)
ROWS = 64


def reach(offset):
    return sum(min(d, SIDE - d) for d in offset)


def opposite(offset):
    return tuple((d + 2) % SIDE for d in offset)


def near(offset):
    other = opposite(offset)
    return (reach(offset), offset) < (reach(other), other)


OFFSETS = sorted(itertools.product(range(SIDE), repeat=3), key=lambda o: -reach(o))
NEAR = [o for o in OFFSETS if near(o)]
NEAR_BACK = [tuple((SIDE - d) % SIDE for d in o) for o in NEAR]
NEAR_PATH = [o for o in NEAR if o[0] % 2 == 0]


class Place:
    def __init__(self):
        self.path, self.tm = lax.axis_index("path"), lax.axis_index("tm")
        self.me = self.path * 4 + self.tm
        z_hi, y, x = self.path // 16, lax.rem(self.path // 4, 4), lax.rem(self.path, 4)
        z, core = z_hi * 2 + self.tm // 2, lax.rem(self.tm, 2)
        self.core, self.chip = core, self.me // 2
        side = range(SIDE)
        zs = [lax.rem(z + d, SIDE) for d in side]
        high = [q // 2 for q in zs]
        self.odd = [lax.rem(q, 2) for q in zs]
        low = [q * 2 for q in self.odd]
        self.zy = [[high[a] * 16 + lax.rem(y + b, SIDE) * 4 for b in side] for a in side]
        self.x = [lax.rem(x + d, SIDE) for d in side]
        self.tms = [[low[a] + core, low[a] + 1 - core] for a in side]
        self.piece_y = [[lax.rem(y + b + 2 * high[a], SIDE) * 4 for b in side] for a in side]
        self.piece_x = [[lax.rem(x + b + 2 * high[a], SIDE) for b in side] for a in side]

    def peer(self, offset, core):
        dz, dy, dx = offset
        return (self.zy[dz][dy] + self.x[dx], self.tms[dz][core])

    def piece(self, offset):
        dz, dy, dx = offset
        return self.piece_y[dz][dy] + self.piece_x[dz][dx]

    def peers(self, offsets, cores=(0, 1)):
        for offset in offsets:
            for core in cores:
                if offset != (0, 0, 0) or core:
                    yield offset, self.peer(offset, core)


def parts(array, count):
    found = []
    for _ in range(count):
        found.append(array.astype(jnp.bfloat16))
        array = array - found[-1].astype(jnp.float32)
    return found


def wait_all(count, ref, sem, place, sent):
    window = ref.at[pl.ds(0, count)]
    copy = pltpu.make_async_remote_copy(
        src_ref=window, dst_ref=window, send_sem=sem, recv_sem=sem,
        device_id=(place.path, place.tm), device_id_type=MESH,
    )
    if sent:
        copy.wait_send()
    else:
        copy.wait_recv()


def kernel(
    inc_hbm, lvl_hbm, time_hbm, value_ref, grad_ref,
    inc, lvl_ref, time_ref, end, end_parts, mask, whole, mine, paired, summed, scattered, arrived, total, gathered,
    table_sem, load_sem, pair_send, pair_recv, scatter_send, scatter_recv, gather_send, gather_recv,
):
    steps_k, width, paths = inc.shape
    step_len = HORIZON / steps_k
    root = jnp.sqrt(jnp.float32(step_len))
    place = Place()
    chips = SIDE**3

    tables = [
        pltpu.make_async_copy(lvl_hbm, lvl_ref, table_sem.at[0]),
        pltpu.make_async_copy(time_hbm, time_ref, table_sem.at[1]),
    ]
    for table in tables:
        table.start()
    loads = [pltpu.make_async_copy(inc_hbm.at[i], inc.at[i], load_sem.at[i]) for i in range(steps_k)]
    for load in loads:
        load.start(priority=1)
    barrier = pltpu.get_barrier_semaphore()
    senders = list(place.peers(OFFSETS, (0,))) + list(place.peers(NEAR_BACK, (1,)))
    for _, peer in senders:
        pl.semaphore_signal(barrier, inc=1, device_id=peer, device_id_type=MESH)

    for table in tables:
        table.wait()

    row_of = lax.broadcasted_iota(jnp.int32, (8, 128), 0)
    own_lvl = lvl_ref[pl.ds(place.me, 1), :].astype(jnp.float32)
    own_time = time_ref[pl.ds(place.me, 1), :].astype(jnp.float32)
    both = jnp.where(row_of == 0, own_lvl, own_time).astype(jnp.bfloat16)
    spread = (
        lax.broadcasted_iota(jnp.int32, (128, paths), 1) // 2
        == lax.broadcasted_iota(jnp.int32, (128, paths), 0)
    ).astype(jnp.float32).astype(jnp.bfloat16)
    per_path = jnp.dot(both, spread, preferred_element_type=jnp.float32)
    lvl, start = per_path[0:1], per_path[1:2]
    start_16 = jnp.broadcast_to(start, (16, paths))
    for i in range(steps_k):
        mask[i] = jnp.where(start_16 <= i, 1.0, 0.0).astype(jnp.bfloat16)

    step_row = lax.broadcasted_iota(jnp.int32, (steps_k, 128), 0)
    counts = [jnp.zeros((steps_k, 128), jnp.int32) for _ in range(LEVELS)]
    for part in range(4):
        packed = jnp.zeros((steps_k, 128), jnp.int32)
        for r in range(part * 32, part * 32 + 32):
            unit = jnp.left_shift(jnp.int32(1), 6 * lvl_ref[pl.ds(r, 1), :])
            packed = packed + jnp.where(time_ref[pl.ds(r, 1), :] == step_row, unit, 0)
        counts = [c + (jnp.right_shift(packed, 6 * n) & 63) for n, c in enumerate(counts)]
    shares = [
        1.0 / (2.0 * jnp.sum(c.astype(jnp.float32), axis=1, keepdims=True)) for c in counts
    ]
    padding = end_parts.shape[1] - width
    end_parts[:, pl.ds(width, padding), :] = jnp.zeros((3, padding, paths), jnp.bfloat16)
    step_at = lax.broadcasted_iota(jnp.int32, (steps_k, paths), 0)
    step_f = step_at.astype(jnp.float32)
    share = jnp.broadcast_to(shares[-1], (steps_k, paths))
    for n in range(LEVELS - 1):
        share = jnp.where(lvl == n, shares[n], share)
    share = jnp.where(start == step_f, share, 0.0)
    scale = root / (HORIZON - step_f[:, 0:1] * step_len)

    def masked_sum(at, rows, slabs, masks):
        terms = []
        for i, m in zip(slabs, masks):
            tiles = [m] * (rows // 16) + ([m[0 : rows % 16]] if rows % 16 else [])
            live = tiles[0] if len(tiles) == 1 else jnp.concatenate(tiles, axis=0)
            terms.append((inc[i, pl.ds(at, rows), :] * live).astype(jnp.float32))
        while len(terms) > 1:
            terms = [sum(terms[n : n + 2][1:], terms[n]) for n in range(0, len(terms), 2)]
        return terms[0]

    chunks, rest = width // ROWS, width % ROWS
    first_slab = 0
    for size in GROUPS[:-1]:
        slabs = range(first_slab, first_slab + size)
        for i in slabs:
            loads[i].wait()
        masks = [mask[i] for i in slabs]

        def add(at, rows, slabs=slabs, masks=masks):
            total_here = masked_sum(at, rows, slabs, masks)
            if slabs[0]:
                end[pl.ds(at, rows), :] += total_here
            else:
                end[pl.ds(at, rows), :] = total_here

        @pl.loop(0, chunks)
        def _(n):
            add(pl.multiple_of(n * ROWS, ROWS), ROWS)

        add(chunks * ROWS, rest)
        first_slab += size

    slabs = range(first_slab, steps_k)
    for i in slabs:
        loads[i].wait()
    masks = [mask[i] for i in slabs]

    def finish(at, rows, squares):
        ended = end[pl.ds(at, rows), :] + masked_sum(at, rows, slabs, masks)
        for n, part in enumerate(parts(ended, 3)):
            end_parts[n, pl.ds(at, rows), :] = part
        return squares + jnp.sum((ended * ended).reshape(rows // 8, 8, paths), axis=0)

    squares = lax.fori_loop(
        0, chunks, lambda n, c: finish(pl.multiple_of(n * ROWS, ROWS), ROWS, c), jnp.zeros((8, paths), jnp.float32)
    )
    squares = finish(chunks * ROWS, rest, squares)
    norm = step_len * jnp.sum(squares, axis=0, keepdims=True)
    end_value = 1.0 / (2.0 + 0.4 * norm / width)
    first = jnp.where(lvl == 0.0, end_value, 0.0)

    def partial_sums(path_total, at, depth):
        select = share * path_total
        weights = parts(select * scale, depth)
        products = []
        for n in range(depth):
            found = lax.dot_general(
                jnp.concatenate(weights[: depth - n], axis=0), end_parts[n],
                (((1,), (1,)), ((), ())), preferred_element_type=jnp.float32,
            )
            products += [(n + m, found[m * steps_k : (m + 1) * steps_k]) for m in range(depth - n)]
        products.sort(key=lambda pair: -pair[0])
        grads = products[0][1]
        for _, product in products[1:]:
            grads = grads + product
        values = jnp.sum(select, axis=1, keepdims=True)
        lane = lax.broadcasted_iota(jnp.int32, (steps_k, 128), 1)
        for c in range(8):
            tile = grads[:, 128 * c : 128 * c + 128]
            if c == width // 128:
                tile = jnp.where(lane == width % 128, values, tile)
            for t, r in itertools.product(range(4), range(2)):
                mine[at, t * 16 + c * 2 + r] = tile[8 * t + 4 * r : 8 * t + 4 * r + 4]

    def scatter(at):
        partner = place.peer((0, 0, 0), 1)
        for k in range(2):
            pltpu.make_async_remote_copy(
                src_ref=mine.at[at, pl.ds((2 * k + 1 - place.core) * 16, 16)], dst_ref=paired.at[at, pl.ds(k * 16, 16)],
                send_sem=pair_send.at[at], recv_sem=pair_recv.at[at],
                device_id=partner, device_id_type=MESH,
            ).start()
        wait_all(32, paired.at[at], pair_recv.at[at], place, False)
        for k in range(2):
            summed[at, pl.ds(k * 16, 16)] = (
                mine[at, pl.ds((2 * k + place.core) * 16, 16)] + paired[at, pl.ds(k * 16, 16)]
            )
        for offset, peer in place.peers(OFFSETS, (0,)):
            pltpu.make_async_remote_copy(
                src_ref=summed.at[at, place.odd[offset[0]] * 16 + place.piece(offset)],
                dst_ref=scattered.at[at, place.chip],
                send_sem=scatter_send.at[at], recv_sem=scatter_recv.at[at],
                device_id=peer, device_id_type=MESH,
            ).start()
        scattered[at, place.chip] = summed[at, place.odd[0] * 16 + place.piece((0, 0, 0))]

    def added(at):
        wait_all(chips - 1, scattered.at[at], scatter_recv.at[at], place, False)
        terms = [scattered[at, n] for n in range(chips)]
        while len(terms) > 1:
            terms = [a + b for a, b in zip(terms[::2], terms[1::2])]
        return terms[0]

    def gather(at, subtotal, offsets, cores, slot, home):
        total[at] = subtotal
        peers = list(place.peers(offsets, cores))
        for _, peer in peers:
            pltpu.make_async_remote_copy(
                src_ref=total.at[at], dst_ref=home.at[slot],
                send_sem=gather_send.at[at], recv_sem=gather_recv.at[at],
                device_id=peer, device_id_type=MESH,
            ).start()
        home[slot] = subtotal
        wait_all(len(peers), home, gather_recv.at[at], place, False)
        return len(peers)

    partial_sums(first, 0, 3)
    pl.semaphore_wait(barrier, len(senders))
    scatter(0)

    fine = jnp.where(lvl == 0.0, 16, jnp.where(lvl == 1.0, 8, jnp.where(lvl == 2.0, 4, jnp.where(lvl == 3.0, 2, 1))))
    on_fine = (step_at & (fine - 1)) == 0
    on_coarse = ((step_at & (2 * fine - 1)) == 0) & (lvl > 0.0)
    fine_f = fine.astype(jnp.float32)
    weight = step_len * (jnp.where(on_fine, fine_f, 0.0) - jnp.where(on_coarse, 2.0 * fine_f, 0.0))
    weight = jnp.where(step_f >= start, weight, 0.0)

    own = place.piece((0, 0, 0))
    sent = gather(0, added(0), NEAR, (0, 1), place.tm * 16 + own, arrived)
    for t, c, r in itertools.product(range(4), range(8), range(2)):
        whole[8 * t + 4 * r : 8 * t + 4 * r + 4, 128 * c : 128 * c + 128] = arrived[t * 16 + c * 2 + r]
    value_one = whole[:, width : width + 1]
    grad_low = whole[:, 0:width].astype(jnp.bfloat16)

    inner = jnp.zeros((steps_k, paths), jnp.float32)
    for i in range(steps_k - 1):
        dots = jnp.dot(grad_low, inc[i], preferred_element_type=jnp.float32)
        inner = inner + jnp.where((start <= i) & (step_at > i), dots, 0.0)
    estimate = value_one + root * inner
    drift = estimate - estimate * estimate * estimate
    second = first + jnp.sum(weight * drift, axis=0, keepdims=True)
    partial_sums(second, 1, 2)
    scatter(1)
    gather_one = sent
    sent = gather(1, added(1), NEAR_PATH, (0,), own, gathered)
    for c, r in itertools.product(range(8), range(2)):
        whole[4 * r : 4 * r + 4, 128 * c : 128 * c + 128] = gathered[c * 2 + r]
    out = whole[0:8, :]
    grad_ref[...] = out[:, 0:width]
    eye = lax.broadcasted_iota(jnp.int32, (8, 8), 0) == lax.broadcasted_iota(jnp.int32, (8, 8), 1)
    value_ref[...] = jnp.sum(jnp.where(eye, out[:, width : width + 1], 0.0), axis=0, keepdims=True)

    for at in range(2):
        wait_all(32, paired.at[at], pair_send.at[at], place, True)
        wait_all(chips - 1, scattered.at[at], scatter_send.at[at], place, True)
    wait_all(gather_one, arrived, gather_send.at[0], place, True)
    wait_all(sent, gathered, gather_send.at[1], place, True)


def shards(increments, level_table, time_table):
    paths, steps_k, width = increments.shape
    slabs = jnp.transpose(increments, (1, 2, 0))
    value, grad = pl.pallas_call(
        kernel,
        out_shape=(
            pltpu.VMEM((1, 8), jnp.float32),
            pltpu.VMEM((8, width), jnp.float32),
        ),
        in_specs=[
            pl.BlockSpec(memory_space=pl.ANY),
            pl.BlockSpec(memory_space=pltpu.HBM),
            pl.BlockSpec(memory_space=pltpu.HBM),
        ],
        out_specs=(pl.BlockSpec(memory_space=pltpu.VMEM), pl.BlockSpec(memory_space=pltpu.VMEM)),
        scratch_shapes=[
            pltpu.VMEM((steps_k, width, paths), jnp.bfloat16),
            pltpu.VMEM((128, 128), jnp.int32),
            pltpu.VMEM((128, 128), jnp.int32),
            pltpu.VMEM((width, paths), jnp.float32),
            pltpu.VMEM((3, 1024, paths), jnp.bfloat16),
            pltpu.VMEM((steps_k, 16, paths), jnp.bfloat16),
            pltpu.VMEM((steps_k, 1024), jnp.float32),
            pltpu.VMEM((2, 64, 4, 128), jnp.float32),
            pltpu.VMEM((2, 32, 4, 128), jnp.float32),
            pltpu.VMEM((2, 32, 4, 128), jnp.float32),
            pltpu.VMEM((2, 64, 4, 128), jnp.float32),
            pltpu.VMEM((64, 4, 128), jnp.float32),
            pltpu.VMEM((2, 4, 128), jnp.float32),
            pltpu.VMEM((16, 4, 128), jnp.float32),
            pltpu.SemaphoreType.DMA((2,)),
            pltpu.SemaphoreType.DMA((steps_k,)),
            pltpu.SemaphoreType.DMA((2,)),
            pltpu.SemaphoreType.DMA((2,)),
            pltpu.SemaphoreType.DMA((2,)),
            pltpu.SemaphoreType.DMA((2,)),
            pltpu.SemaphoreType.DMA((2,)),
            pltpu.SemaphoreType.DMA((2,)),
        ],
        compiler_params=pltpu.CompilerParams(
            collective_id=0, has_side_effects=True, vmem_limit_bytes=67043328 - 64 * 1024
        ),
    )(slabs, level_table.reshape(128, 128), time_table.reshape(128, 128))
    return (value.reshape(8), grad)


def solution(mesh):
    placed = (P(("path", "tm"), None, None), P(), P())
    return jax.shard_map(
        shards, mesh=mesh, in_specs=placed, out_specs=(P("tm"), P("tm", None)), check_vma=False
    )
```

time: 43.3 us -> 40.3 us (0.931)
  local copies, waits for them, and re-layouts: 2.8 us -> 1.13 us
  Pallas kernels: 39.6 us -> 38.1 us
    unnamed x6 -> x2, local copies, waits for them, and re-layouts: 2.8 us -> 1.13 us
    pallas_call x1, Pallas kernels: 39.6 us -> 38.1 us  [shards(): pl.pallas_call(kernel, out_shape=(pltpu.VMEM((1, 8), jnp.float32), pltpu....]
where the time goes in v2:
time: 40.3 us; the launch traced here: 39.9 us
  Pallas kernels  38.1 us (95%)
  local copies, waits for them, and re-layouts  1.13 us (3%)
  between operations  0.64 us (2%)
    pallas_call x1, Pallas kernels, shards(): pl.pallas_call(kernel, out_shape=(pltpu.VMEM((1, 8), jnp.float32), pltpu....  38.1 us
    unnamed x2, local copies, waits for them, and re-layouts  1.13 us

profile of v2, /device:TPU:1, one launch (start us, length us, event | category | flops | bytes accessed | tf_op | source)
XLA Modules:
  0.0 39.9 jit_solution(16021849846254025890)
XLA Ops:
  0.6 38.1 %shard_map.50 = (f32[1,8]{1,0:T(1,128)S(1)}, f32[8,1000]{1,0:T(8,128)S(1)}) custom-call(bf16[32,1000,256]{2,1,0:T(8,128)(2,1)} %bitcast.5, s32[128,128]{1,0:T(8,128)} %bitcast.6, s32[128,128]{1,0:T(8,128)} %bitcast.7), custom_call_target="tpu_custom_call" | custom-call | tf_op jit(solution)/shard_map/pallas_call | solution.py:317
  38.8 0.5 %copy.7 = f32[8]{0:T(128)} copy(f32[8]{0:T(128)S(1)} %bitcast.4) | data formatting | bytes 64
  39.3 0.6 %copy.8 = f32[8,1000]{1,0:T(8,128)} copy(f32[8,1000]{1,0:T(8,128)S(1)} %get-tuple-element.7) | data formatting | bytes 64000
